TPU v7x, 32 devices: a whole 2x2x4 slice. The times are simulated.
32 devices in a mesh: row: 4 (over x, core), col: 8 (over z, y).
Axes of the slice: x: 2, y: 2, z: 4, core: 2. Of those that a mesh axis runs over, the one named last changes fastest.
Arguments:
- rows: bfloat16 [1024, 4096], P(('row', 'col')), may hold values from -6 to 6
- task_ids: int32 [1024], P(('row', 'col')), may hold values from 0 to 8, as said below
- task_embed: bfloat16 [8, 4096], replicated, may hold values from -6 to 6
- norm_gain: float32 [4, 4096], replicated, may hold values from 0.1 to 1.9
- layer_weight: bfloat16 [4, 4096, 4096], P(None, None, 'col'), may hold values from -0.09375 to 0.09375
Outputs:
- packed_out: bfloat16 [1024, 4096], P('row', 'col')
Inputs may be any that keep to these rules, and one draw needn't show every extreme that they name: `task_ids`: 8 marks an empty row, smaller values name a task.
All inputs are finite; a program needn't handle non-finite values.
Results may differ from a plain program's by a relative error of at most 0.008.
Values may be sent and summed in bfloat16 or wider, within the bound.
A program may use at most 128 MiB of HBM per device.

v0:
```python
import jax
import jax.numpy as jnp
from jax import lax
from jax.sharding import PartitionSpec as P

epsilon = 1e-06


def entering(part, axis, combine, identity):
    place = lax.axis_index(axis)
    gathered = lax.all_gather(part, axis)
    state = jnp.zeros_like(part) + jnp.asarray(identity, part.dtype)

    def one(hop, state):
        return combine(state, lax.dynamic_index_in_dim(gathered, hop, 0, False))

    return lax.fori_loop(0, place, one, state)


def add_counts(earlier, later):
    return earlier + later


def activate_rows(hidden, gain):
    total_rows = hidden.shape[0]
    width = hidden.shape[1]
    block_rows = min(512, total_rows)

    def one_block(block):
        values = block.astype(jnp.float32)
        inverse_rms = lax.rsqrt(jnp.mean(values * values, axis=1, keepdims=True) + epsilon)
        return jax.nn.silu(values * inverse_rms * gain[None, :]).astype(jnp.bfloat16)

    blocks = hidden.reshape(total_rows // block_rows, block_rows, width)
    return lax.map(one_block, blocks).reshape(total_rows, width)


def shards(rows, task_ids, task_embed, norm_gain, layer_weight):
    row_count = rows.shape[0]
    width = rows.shape[1]
    task_count = task_embed.shape[0]
    row_devices = lax.axis_size("row")
    col_devices = lax.axis_size("col")
    capacity = row_count // row_devices + task_count
    slots_group = row_count * col_devices
    task_range = jnp.arange(task_count, dtype=jnp.int32)
    member = (task_ids[:, None] == task_range[None, :]).astype(jnp.int32)
    counts = jnp.sum(member, axis=0)
    zero_counts = jnp.zeros_like(counts)
    before_col = entering(counts, "col", add_counts, zero_counts)
    row_total = lax.psum(counts, "col")
    before_row = entering(row_total, "row", add_counts, zero_counts)
    totals = lax.psum(row_total, "row")
    before = before_row + before_col
    task_base = jnp.cumsum(totals) - totals
    positions = jnp.arange(row_count, dtype=jnp.int32)
    earlier_mask = positions[None, :] < positions[:, None]
    same_task = task_ids[:, None] == task_ids[None, :]
    task_rank = jnp.sum((same_task & earlier_mask).astype(jnp.int32), axis=1)
    row_live = task_ids < task_count
    packed_pos = (
        jnp.sum(member * (task_base + before)[None, :], axis=1).astype(jnp.int32) + task_rank
    )
    target_row = packed_pos % row_devices
    slot_index = packed_pos // row_devices
    before_pos = packed_pos[None, :] < packed_pos[:, None]
    same_target = (target_row[:, None] == target_row[None, :]) & row_live[None, :]
    within = jnp.sum((same_target & before_pos).astype(jnp.int32), axis=1)
    send_at = jnp.where(row_live, target_row * capacity + within, -1)
    buffer_range = jnp.arange(row_devices * capacity, dtype=jnp.int32)
    select = buffer_range[:, None] == send_at[None, :]
    send_rows = jnp.dot(
        select.astype(jnp.bfloat16), rows, preferred_element_type=jnp.float32
    ).astype(jnp.bfloat16)
    send_rows = send_rows.reshape(row_devices, capacity, width)
    send_slots = jnp.sum(jnp.where(select, slot_index[None, :] + 1, 0), axis=1) - 1
    send_slots = send_slots.reshape(row_devices, capacity)
    got_rows, got_slots = (
        lax.all_to_all(send_rows, "row", split_axis=0, concat_axis=0, tiled=True),
        lax.all_to_all(send_slots, "row", split_axis=0, concat_axis=0, tiled=True),
    )
    got_rows = got_rows.reshape(row_devices * capacity, width)
    got_slots = got_slots.reshape(row_devices * capacity)
    slot_range = jnp.arange(slots_group, dtype=jnp.int32)
    piece_rows = lax.all_gather(got_rows, "col", axis=0, tiled=True)
    piece_slots = lax.all_gather(got_slots, "col", axis=0, tiled=True)
    safe_slots = jnp.where(piece_slots >= 0, piece_slots, slots_group).astype(jnp.int32)
    placed = (
        jnp.zeros((slots_group, width), jnp.bfloat16).at[safe_slots].set(piece_rows, mode="drop")
    )
    group_index = lax.axis_index("row")
    slot_pos = slot_range * row_devices + group_index
    in_task = (slot_pos[:, None] >= task_base[None, :]) & (
        slot_pos[:, None] < (task_base + totals)[None, :]
    )
    task_term = jnp.dot(
        in_task.astype(jnp.bfloat16), task_embed, preferred_element_type=jnp.float32
    )
    hidden = (placed.astype(jnp.float32) + task_term).astype(jnp.bfloat16)
    part_width = width // col_devices
    column = lax.axis_index("col") * part_width
    layers = layer_weight.shape[0]
    result = hidden
    for layer_index in range(layers):
        active = activate_rows(hidden, norm_gain[layer_index])
        update = jnp.dot(active, layer_weight[layer_index], preferred_element_type=jnp.float32)
        own_cols = lax.dynamic_slice_in_dim(hidden, column, part_width, 1).astype(jnp.float32)
        result = (own_cols + update).astype(jnp.bfloat16)
        if layer_index + 1 < layers:
            hidden = lax.all_gather(result, "col", axis=1, tiled=True)
    return result


def solution(mesh):
    return jax.shard_map(
        shards,
        mesh=mesh,
        in_specs=(P(("row", "col"), None), P(("row", "col")), P(), P(), P(None, None, "col")),
        out_specs=P("row", "col"),
        check_vma=False,
    )
```

profile of v0, /device:TPU:0, one launch (start us, length us, event | category | flops | bytes accessed | tf_op | source)
XLA Modules:
  0.0 303.9 jit_solution(6992512767991493794)
XLA Ops:
  6.5 0.8 convert_reduce_fusion.2
  7.4 0.9 convert_reduce_fusion.1
  8.3 0.7 broadcast_compare_fusion
  8.9 1.3 dynamic-slice.5
  10.9 0.2 dynamic-update-slice.1
  11.1 13.1 %all-reduce.3 = (s32[8]{0:T(128)S(1)}, s32[64]{0:T(128)S(1)}) all-reduce(s32[8]{0:T(128)S(1)} %convert_reduce_fusion.2, s32[64]{0:T(128)S(1)} %dynamic-update-slice.1), channel_id=1, replica_groups=mesh['row'=4,'col'=8] {'col'}, use_global_device_ids=true, to_apply=%region_1.2 | all-reduce | flops 72 | bytes 576 | tf_op jit(solution)/shard_map/psum | solution.py:51
  24.2 1.2 dynamic-slice.4
  26.1 0.2 dynamic-update-slice
  26.4 4.9 %all-reduce.4 = (s32[8]{0:T(128)S(1)}, s32[32]{0:T(128)S(1)}) all-reduce(s32[8]{0:T(128)S(1)} %get-tuple-element.117, s32[32]{0:T(128)S(1)} %dynamic-update-slice), channel_id=1, replica_groups=mesh['row'=4,'col'=8] {'row'}, use_global_device_ids=true, to_apply=%region_2.3 | all-reduce | flops 40 | bytes 320 | tf_op jit(solution)/shard_map/psum | solution.py:53
  31.3 0.1 reshape.226
  31.3 0.1 reshape.227
  31.4 0.2 reduce-window.8
  31.6 0.7 select_reduce_fusion.1
  32.4 0.2 convert_reduce_fusion
  32.6 0.7 add_select_fusion
  33.2 0.4 convolution_convert_fusion
  33.7 11.9 %all_to_all.11 = bf16[4,16,4096]{2,1,0:T(8,128)(2,1)} all-to-all(bf16[4,16,4096]{2,1,0:T(8,128)(2,1)S(1)} %bitcast.53), channel_id=1, replica_groups=mesh['row'=4,'col'=8] {'row'}, dimensions={0} | all-to-all | bytes 1048576 | tf_op jit(solution)/shard_map/all_to_all | solution.py:79
  45.6 0.0 all-gather.7.cloned.1.call-update
  45.6 0.1 select_reduce_fusion
  45.7 0.7 sub.18
  46.3 3.2 %all-to-all-start = ((s32[4,1,16]{2,1,0:T(1,128)}), s32[4,1,16]{2,1,0:T(1,128)S(1)}, u32[]{:S(2)}, u32[]{:S(2)}) async-start(s32[4,1,16]{2,1,0:T(1,128)} %bitcast.6), calls=%async_computation | async-start | bytes 4096 | tf_op jit(solution)/shard_map/all_to_all | solution.py:80
  49.6 0.0 all-gather.9.cloned.1.call-start
  50.3 1.1 fusion.112
  51.3 1.9 all-to-all-done
  53.2 0.5 broadcast.253
  53.8 0.7 reduce.3
  54.4 0.1 reshape.235
  54.5 0.2 dynamic-update-slice.2
  54.7 9.3 %all-reduce.2 = s32[512]{0:T(512)S(1)} all-reduce(s32[512]{0:T(512)S(1)} %dynamic-update-slice.2), channel_id=1, replica_groups=mesh['row'=4,'col'=8] {'col'}, use_global_device_ids=true, to_apply=%add.2 | all-reduce | flops 512 | bytes 4096
  64.0 52.0 %all-gather.7.cloned.1.call-done = bf16[512,4096]{1,0:T(8,128)(2,1)} async-done(((bf16[64,4096]{1,0:T(8,128)(2,1)}), bf16[512,4096]{1,0:T(8,128)(2,1)}) %all-gather.7.cloned.1.call-update) | async-done | bytes 4194320 | tf_op jit(solution)/shard_map/all_gather | solution.py:85
  116.0 8.2 %scatter_custom_fusion = bf16[256,4096]{1,0:T(8,128)(2,1)S(1)} fusion(s32[512]{0:T(512)S(1)} %compare_select_fusion, bf16[512,4096]{1,0:T(8,128)(2,1)} %all-gather.7.cloned.1.call-done, bf16[]{:T(256)} %constant.131.clone.1), kind=kCustom, calls=%fused_computation.74 | custom fusion | bytes 2097664 | tf_op jit(solution)/shard_map/scatter | solution.py:89
  124.3 0.0 copy-done.1
  124.3 1.0 fusion.1
  125.3 4.4 %fusion.92 = bf16[256,512]{1,0:T(8,128)(2,1)} fusion(bf16[4,4096,512]{2,1,0:T(8,128)(2,1)} %param.13, bf16[256,4096]{1,0:T(8,128)(2,1)S(1)} %get-tuple-element.130, f32[4096]{0:T(1024)S(1)} %bitcast.57, f32[256]{0:T(256)S(1)} %add_rsqrt_fusion.3, s32[]{:T(128)S(6)} %select_n.59), kind=kOutput, calls=%fused_computation.73 | convolution fusion | flops 1082523648 | bytes 6833156 | tf_op jit(solution)/shard_map/dot_general | solution.py:106
  129.7 0.0 all-gather.9.cloned.1.call-update
  129.7 0.2 all-gather.11.cloned.1.call-start
  129.9 48.8 %all-gather.9.cloned.1.call-done = bf16[256,4096]{1,0:T(8,128)(2,1)} async-done(((bf16[256,512]{1,0:T(8,128)(2,1)}), bf16[256,4096]{1,0:T(8,128)(2,1)}) %all-gather.9.cloned.1.call-update) | async-done | bytes 2097168 | tf_op jit(solution)/shard_map/all_gather | solution.py:110
  178.7 2.1 fusion.9
  180.8 5.0 %fusion.87 = bf16[256,512]{1,0:T(8,128)(2,1)} fusion(bf16[4,4096,512]{2,1,0:T(8,128)(2,1)} %param.13, bf16[256,4096]{1,0:T(8,128)(2,1)} %all-gather.9.cloned.1.call-done, f32[4096]{0:T(1024)S(1)} %bitcast.56, f32[256]{0:T(256)S(1)} %add_rsqrt_fusion.2, s32[]{:T(128)S(6)} %select_n.59), kind=kOutput, calls=%fused_computation.72 | convolution fusion | flops 1082523648 | bytes 6833156 | tf_op jit(solution)/shard_map/dot_general | solution.py:106
  185.8 0.0 all-gather.11.cloned.1.call-update
  185.8 0.0 all-gather.13.cloned.1.call-start
  185.8 48.6 %all-gather.11.cloned.1.call-done = bf16[256,4096]{1,0:T(8,128)(2,1)} async-done(((bf16[256,512]{1,0:T(8,128)(2,1)}), bf16[256,4096]{1,0:T(8,128)(2,1)}) %all-gather.11.cloned.1.call-update) | async-done | bytes 2097168 | tf_op jit(solution)/shard_map/all_gather | solution.py:110
  234.5 2.1 fusion.17
  236.6 5.0 %fusion.82 = bf16[256,512]{1,0:T(8,128)(2,1)} fusion(bf16[4,4096,512]{2,1,0:T(8,128)(2,1)} %param.13, bf16[256,4096]{1,0:T(8,128)(2,1)} %all-gather.11.cloned.1.call-done, f32[4096]{0:T(1024)S(1)} %bitcast.55, f32[256]{0:T(256)S(1)} %add_rsqrt_fusion.1, s32[]{:T(128)S(6)} %select_n.59), kind=kOutput, calls=%fused_computation.71 | convolution fusion | flops 1082523648 | bytes 6833156 | tf_op jit(solution)/shard_map/dot_general | solution.py:106
  241.5 0.0 all-gather.13.cloned.1.call-update
  241.6 48.8 %all-gather.13.cloned.1.call-done = bf16[256,4096]{1,0:T(8,128)(2,1)} async-done(((bf16[256,512]{1,0:T(8,128)(2,1)}), bf16[256,4096]{1,0:T(8,128)(2,1)}) %all-gather.13.cloned.1.call-update) | async-done | bytes 2097168 | tf_op jit(solution)/shard_map/all_gather | solution.py:110
  290.3 2.1 fusion.25
  292.4 5.0 %fusion.77 = bf16[256,512]{1,0:T(8,128)(2,1)} fusion(bf16[4,4096,512]{2,1,0:T(8,128)(2,1)} %param.13, bf16[256,4096]{1,0:T(8,128)(2,1)} %all-gather.13.cloned.1.call-done, f32[4096]{0:T(1024)S(1)} %bitcast.54, f32[256]{0:T(256)S(1)} %add_rsqrt_fusion, s32[]{:T(128)S(6)} %select_n.59), kind=kOutput, calls=%fused_computation.70 | convolution fusion | flops 1082523648 | bytes 6833156 | tf_op jit(solution)/shard_map/dot_general | solution.py:106
  (20 shorter events, 0.1 us)
Async XLA Ops:
  6.5 26.7 %copy-start = (bf16[32,4096]{1,0:T(8,128)(2,1)S(1)}, bf16[32,4096]{1,0:T(8,128)(2,1)}, u32[]{:S(2)}) copy-start(bf16[32,4096]{1,0:T(8,128)(2,1)} %param.9) | copy-start | bytes 786436
  6.5 117.7 %copy-start.1 = (bf16[8,4096]{1,0:T(8,128)(2,1)S(1)}, bf16[8,4096]{1,0:T(8,128)(2,1)}, u32[]{:S(2)}) copy-start(bf16[8,4096]{1,0:T(8,128)(2,1)} %param.11) | copy-start | bytes 196612
  6.5 109.5 %all-gather.7.cloned.1.call-start = ((), (), s32[]{:S(2)}) async-start(), calls=%async_computation.2 | async-start | bytes 4718592 | tf_op jit(solution)/shard_map/all_gather | solution.py:85
  46.3 6.9 %all-to-all-start = ((s32[4,1,16]{2,1,0:T(1,128)}), s32[4,1,16]{2,1,0:T(1,128)S(1)}, u32[]{:S(2)}, u32[]{:S(2)}) async-start(s32[4,1,16]{2,1,0:T(1,128)} %bitcast.6), calls=%async_computation | async-start | bytes 4096 | tf_op jit(solution)/shard_map/all_to_all | solution.py:80
  49.6 129.1 %all-gather.9.cloned.1.call-start = ((), (), s32[]{:S(2)}) async-start(), calls=%async_computation.3 | async-start | bytes 2359296 | tf_op jit(solution)/shard_map/all_gather | solution.py:110
  129.7 104.8 %all-gather.11.cloned.1.call-start = ((), (), s32[]{:S(2)}) async-start(), calls=%async_computation.4 | async-start | bytes 2359296 | tf_op jit(solution)/shard_map/all_gather | solution.py:110
  185.8 104.5 %all-gather.13.cloned.1.call-start = ((), (), s32[]{:S(2)}) async-start(), calls=%async_computation.5 | async-start | bytes 2359296 | tf_op jit(solution)/shard_map/all_gather | solution.py:110
Sparse Core Ops, SparseCore 0:
  45.7 70.2 all-gather.6
  129.8 48.8 all-gather.8
  185.9 48.5 all-gather.10
  241.7 48.5 all-gather.12
where the time goes:
time: 304 us
  waiting for transfers between devices  200 us (66%)
  blocking collectives  39.2 us (13%)
  matrix products  20.7 us (7%)
  between operations  15.1 us (5%)
  local copies, waits for them, and re-layouts  13.9 us (5%)
  other arithmetic  11.3 us (4%)
  starting transfers between devices  3.53 us (1%)
    all_gather x3, waiting for transfers between devices, shards(): hidden = lax.all_gather(result, 'col', axis=1, tiled=True)  146 us
    all_gather x1, waiting for transfers between devices, shards(): piece_rows = lax.all_gather(got_rows, 'col', axis=0, tiled=True)  52 us
    dot_general x4, matrix products, shards(): jnp.dot(active, layer_weight[layer_index], preferred_element_type=jnp.flo...  19.3 us
    psum x1, blocking collectives, shards(): row_total = lax.psum(counts, 'col')  13.1 us
    all_to_all x1, blocking collectives, shards(): lax.all_to_all(send_rows, 'row', split_axis=0, concat_axis=0, tiled=True)  11.9 us
    unnamed x1, blocking collectives  9.34 us
    scatter x1, local copies, waits for them, and re-layouts, shards(): jnp.zeros((slots_group, width), jnp.bfloat16).at[safe_slots]  8.22 us
    reduce_sum x3, other arithmetic, one_block(): jnp.mean(values * values, axis=1, keepdims=True) + epsilon  6.25 us
  transfers between devices with their start and end apart: 5, of which 5 were waited for; matrix products, arithmetic and copies ran while one was open for 1% of the time, Pallas kernels for 0%

commit v1 on v0

--- a/solution.py
+++ b/solution.py
@@ -82,7 +82,8 @@
     got_rows = got_rows.reshape(row_devices * capacity, width)
     got_slots = got_slots.reshape(row_devices * capacity)
     slot_range = jnp.arange(slots_group, dtype=jnp.int32)
-    piece_rows = lax.all_gather(got_rows, "col", axis=0, tiled=True)
+    outgoing = jnp.stack([got_rows] * lax.axis_size("col"))
+    piece_rows = jnp.concatenate(lax.all_to_all(outgoing, "col", 0, 0), axis=0)
     piece_slots = lax.all_gather(got_slots, "col", axis=0, tiled=True)
     safe_slots = jnp.where(piece_slots >= 0, piece_slots, slots_group).astype(jnp.int32)
     placed = (

time: 304 us -> 341 us (1.12)
  blocking collectives: 39.2 us -> 120 us
  waiting for transfers between devices: 200 us -> 149 us
  starting transfers between devices: 3.53 us -> 8.2 us
    unnamed x1, blocking collectives: 9.34 us -> 91 us
    all_gather x1 -> x0, waiting for transfers between devices: 52 us -> none  [shards(): piece_rows = lax.all_gather(got_rows, 'col', axis=0, tiled=True)]
    all_to_all x0 -> x1, starting transfers between devices: none -> 4.68 us  [shards(): piece_rows = jnp.concatenate(lax.all_to_all(outgoing, 'col', 0, 0), axis=0)]
  transfers between devices with their start and end apart: 5 -> 5, of which waited for: 5 -> 4; matrix products, arithmetic and copies ran while one was open for 1% -> 1% of each run, Pallas kernels for 0% -> 0%
where the time goes in v1:
time: 341 us; the launch traced here: 340 us
  waiting for transfers between devices  149 us (44%)
  blocking collectives  120 us (35%)
  matrix products  20.6 us (6%)
  local copies, waits for them, and re-layouts  15.4 us (5%)
  between operations  15.1 us (4%)
  other arithmetic  11.2 us (3%)
  starting transfers between devices  8.2 us (2%)
    all_gather x3, waiting for transfers between devices, shards(): hidden = lax.all_gather(result, 'col', axis=1, tiled=True)  146 us
    unnamed x1, blocking collectives  91 us
    dot_general x4, matrix products, shards(): jnp.dot(active, layer_weight[layer_index], preferred_element_type=jnp.flo...  19.2 us
    psum x1, blocking collectives, shards(): row_total = lax.psum(counts, 'col')  13.1 us
    all_to_all x1, blocking collectives, shards(): lax.all_to_all(send_rows, 'row', split_axis=0, concat_axis=0, tiled=True)  11.2 us
    scatter x1, local copies, waits for them, and re-layouts, shards(): jnp.zeros((slots_group, width), jnp.bfloat16).at[safe_slots]  8.22 us
  transfers between devices with their start and end apart: 5, of which 4 were waited for; matrix products, arithmetic and copies ran while one was open for 1% of the time, Pallas kernels for 0%

profile of v1, /device:TPU:0, one launch (start us, length us, event | category | flops | bytes accessed | tf_op | source)
XLA Modules:
  0.0 340.1 jit_solution(14075383895532243169)
XLA Ops:
  6.5 0.8 convert_reduce_fusion.2
  7.4 0.9 convert_reduce_fusion.1
  8.3 0.7 broadcast_compare_fusion
  8.9 1.2 dynamic-slice.5
  10.8 0.2 dynamic-update-slice.1
  11.1 13.1 %all-reduce.3 = (s32[8]{0:T(128)S(1)}, s32[64]{0:T(128)S(1)}) all-reduce(s32[8]{0:T(128)S(1)} %convert_reduce_fusion.2, s32[64]{0:T(128)S(1)} %dynamic-update-slice.1), channel_id=1, replica_groups=mesh['row'=4,'col'=8] {'col'}, use_global_device_ids=true, to_apply=%region_1.2 | all-reduce | flops 72 | bytes 576 | tf_op jit(solution)/shard_map/psum | solution.py:51
  24.1 1.2 dynamic-slice.4
  26.0 0.2 dynamic-update-slice
  26.3 4.9 %all-reduce.4 = (s32[8]{0:T(128)S(1)}, s32[32]{0:T(128)S(1)}) all-reduce(s32[8]{0:T(128)S(1)} %get-tuple-element.117, s32[32]{0:T(128)S(1)} %dynamic-update-slice), channel_id=1, replica_groups=mesh['row'=4,'col'=8] {'row'}, use_global_device_ids=true, to_apply=%region_2.3 | all-reduce | flops 40 | bytes 320 | tf_op jit(solution)/shard_map/psum | solution.py:53
  31.2 0.1 reshape.228
  31.3 0.1 reshape.229
  31.4 0.2 reduce-window.8
  31.6 0.7 select_reduce_fusion.1
  32.3 0.2 convert_reduce_fusion
  32.5 0.7 add_select_fusion
  33.2 0.1 select_reduce_fusion
  33.3 0.7 sub.18
  33.9 3.2 all-to-all-start
  37.2 0.4 convolution_convert_fusion
  37.6 3.2 all-to-all-done
  40.8 11.2 %all_to_all.16 = bf16[4,16,4096]{2,1,0:T(8,128)(2,1)S(1)} all-to-all(bf16[4,16,4096]{2,1,0:T(8,128)(2,1)S(1)} %bitcast.54), channel_id=1, replica_groups=mesh['row'=4,'col'=8] {'row'}, dimensions={0} | all-to-all | bytes 1048576 | tf_op jit(solution)/shard_map/all_to_all | solution.py:79
  52.0 2.5 stack.3
  54.5 4.7 %all-to-all-start.2 = ((bf16[8,64,4096]{2,1,0:T(8,128)(2,1)}), bf16[8,64,4096]{2,1,0:T(8,128)(2,1)}, u32[]{:S(2)}, u32[]{:S(2)}) async-start(bf16[8,64,4096]{2,1,0:T(8,128)(2,1)} %stack.3), calls=%async_computation.2 | async-start | bytes 8388608 | tf_op jit(solution)/shard_map/all_to_all | solution.py:86
  59.2 0.0 all-gather.6.cloned.1.call-start
  60.0 0.5 broadcast.254
  60.5 0.7 reduce.3
  61.2 0.1 reshape.237
  61.2 0.2 dynamic-update-slice.2
  61.4 91.0 %all-reduce.2 = s32[512]{0:T(512)S(1)} all-reduce(s32[512]{0:T(512)S(1)} %dynamic-update-slice.2), channel_id=1, replica_groups=mesh['row'=4,'col'=8] {'col'}, use_global_device_ids=true, to_apply=%add.2 | all-reduce | flops 512 | bytes 4096
  152.5 0.0 all-to-all-done.2
  152.5 8.2 %scatter_custom_fusion = bf16[256,4096]{1,0:T(8,128)(2,1)S(1)} fusion(s32[512]{0:T(512)S(1)} %compare_select_fusion, bf16[512,4096]{1,0:T(8,128)(2,1)} %bitcast.10, bf16[]{:T(256)} %constant.131.clone.1), kind=kCustom, calls=%fused_computation.74 | custom fusion | bytes 2097664 | tf_op jit(solution)/shard_map/scatter | solution.py:90
  160.7 0.0 copy-done.2
  160.7 1.0 fusion.1
  161.7 4.3 %fusion.92 = bf16[256,512]{1,0:T(8,128)(2,1)} fusion(bf16[4,4096,512]{2,1,0:T(8,128)(2,1)} %param.13, bf16[256,4096]{1,0:T(8,128)(2,1)S(1)} %get-tuple-element.130, f32[4096]{0:T(1024)S(1)} %bitcast.58, f32[256]{0:T(256)S(1)} %add_rsqrt_fusion.3, s32[]{:T(128)S(6)} %select_n.59), kind=kOutput, calls=%fused_computation.73 | convolution fusion | flops 1082523648 | bytes 6833156 | tf_op jit(solution)/shard_map/dot_general | solution.py:107
  166.0 0.0 all-gather.6.cloned.1.call-update
  166.0 0.2 all-gather.8.cloned.1.call-start
  166.3 48.6 %all-gather.6.cloned.1.call-done = bf16[256,4096]{1,0:T(8,128)(2,1)} async-done(((bf16[256,512]{1,0:T(8,128)(2,1)}), bf16[256,4096]{1,0:T(8,128)(2,1)}) %all-gather.6.cloned.1.call-update) | async-done | bytes 2097168 | tf_op jit(solution)/shard_map/all_gather | solution.py:111
  214.9 2.1 fusion.9
  217.0 5.0 %fusion.87 = bf16[256,512]{1,0:T(8,128)(2,1)} fusion(bf16[4,4096,512]{2,1,0:T(8,128)(2,1)} %param.13, bf16[256,4096]{1,0:T(8,128)(2,1)} %all-gather.6.cloned.1.call-done, f32[4096]{0:T(1024)S(1)} %bitcast.57, f32[256]{0:T(256)S(1)} %add_rsqrt_fusion.2, s32[]{:T(128)S(6)} %select_n.59), kind=kOutput, calls=%fused_computation.72 | convolution fusion | flops 1082523648 | bytes 6833156 | tf_op jit(solution)/shard_map/dot_general | solution.py:107
  222.0 0.0 all-gather.8.cloned.1.call-update
  222.0 0.0 all-gather.10.cloned.1.call-start
  222.0 48.6 %all-gather.8.cloned.1.call-done = bf16[256,4096]{1,0:T(8,128)(2,1)} async-done(((bf16[256,512]{1,0:T(8,128)(2,1)}), bf16[256,4096]{1,0:T(8,128)(2,1)}) %all-gather.8.cloned.1.call-update) | async-done | bytes 2097168 | tf_op jit(solution)/shard_map/all_gather | solution.py:111
  270.7 2.1 fusion.17
  272.8 5.0 %fusion.82 = bf16[256,512]{1,0:T(8,128)(2,1)} fusion(bf16[4,4096,512]{2,1,0:T(8,128)(2,1)} %param.13, bf16[256,4096]{1,0:T(8,128)(2,1)} %all-gather.8.cloned.1.call-done, f32[4096]{0:T(1024)S(1)} %bitcast.56, f32[256]{0:T(256)S(1)} %add_rsqrt_fusion.1, s32[]{:T(128)S(6)} %select_n.59), kind=kOutput, calls=%fused_computation.71 | convolution fusion | flops 1082523648 | bytes 6833156 | tf_op jit(solution)/shard_map/dot_general | solution.py:107
  277.7 0.0 all-gather.10.cloned.1.call-update
  277.8 48.8 %all-gather.10.cloned.1.call-done = bf16[256,4096]{1,0:T(8,128)(2,1)} async-done(((bf16[256,512]{1,0:T(8,128)(2,1)}), bf16[256,4096]{1,0:T(8,128)(2,1)}) %all-gather.10.cloned.1.call-update) | async-done | bytes 2097168 | tf_op jit(solution)/shard_map/all_gather | solution.py:111
  326.5 2.1 fusion.25
  328.6 5.0 %fusion.77 = bf16[256,512]{1,0:T(8,128)(2,1)} fusion(bf16[4,4096,512]{2,1,0:T(8,128)(2,1)} %param.13, bf16[256,4096]{1,0:T(8,128)(2,1)} %all-gather.10.cloned.1.call-done, f32[4096]{0:T(1024)S(1)} %bitcast.55, f32[256]{0:T(256)S(1)} %add_rsqrt_fusion, s32[]{:T(128)S(6)} %select_n.59), kind=kOutput, calls=%fused_computation.70 | convolution fusion | flops 1082523648 | bytes 6833156 | tf_op jit(solution)/shard_map/dot_general | solution.py:107
  (22 shorter events, 0.1 us)
Async XLA Ops:
  6.5 30.6 %copy-start = (bf16[32,4096]{1,0:T(8,128)(2,1)S(1)}, bf16[32,4096]{1,0:T(8,128)(2,1)}, u32[]{:S(2)}) copy-start(bf16[32,4096]{1,0:T(8,128)(2,1)} %param.9) | copy-start | bytes 786436
  33.9 6.9 %all-to-all-start = ((s32[4,1,16]{2,1,0:T(1,128)}), s32[4,1,16]{2,1,0:T(1,128)S(1)}, u32[]{:S(2)}, u32[]{:S(2)}) async-start(s32[4,1,16]{2,1,0:T(1,128)} %bitcast.6), calls=%async_computation | async-start | bytes 4096 | tf_op jit(solution)/shard_map/all_to_all | solution.py:80
  54.5 5.4 %copy-start.1 = (f32[4,4096]{1,0:T(4,128)S(1)}, f32[4,4096]{1,0:T(4,128)}, u32[]{:S(2)}) copy-start(f32[4,4096]{1,0:T(4,128)} %param.12) | copy-start | bytes 196612
  54.5 106.2 %copy-start.2 = (bf16[8,4096]{1,0:T(8,128)(2,1)S(1)}, bf16[8,4096]{1,0:T(8,128)(2,1)}, u32[]{:S(2)}) copy-start(bf16[8,4096]{1,0:T(8,128)(2,1)} %param.11) | copy-start | bytes 196612
  54.5 97.9 %all-to-all-start.2 = ((bf16[8,64,4096]{2,1,0:T(8,128)(2,1)}), bf16[8,64,4096]{2,1,0:T(8,128)(2,1)}, u32[]{:S(2)}, u32[]{:S(2)}) async-start(bf16[8,64,4096]{2,1,0:T(8,128)(2,1)} %stack.3), calls=%async_computation.2 | async-start | bytes 8388608 | tf_op jit(solution)/shard_map/all_to_all | solution.py:86
  59.2 155.7 %all-gather.6.cloned.1.call-start = ((), (), s32[]{:S(2)}) async-start(), calls=%async_computation.3 | async-start | bytes 2359296 | tf_op jit(solution)/shard_map/all_gather | solution.py:111
  166.0 104.6 %all-gather.8.cloned.1.call-start = ((), (), s32[]{:S(2)}) async-start(), calls=%async_computation.4 | async-start | bytes 2359296 | tf_op jit(solution)/shard_map/all_gather | solution.py:111
  222.0 104.5 %all-gather.10.cloned.1.call-start = ((), (), s32[]{:S(2)}) async-start(), calls=%async_computation.5 | async-start | bytes 2359296 | tf_op jit(solution)/shard_map/all_gather | solution.py:111
Sparse Core Ops, SparseCore 0:
  166.2 48.6 all-gather.5
  222.1 48.5 all-gather.7
  277.9 48.5 all-gather.9
